TPU v7x, 32 devices: a whole 2x2x4 slice. The times are simulated.
32 devices in a mesh: wide: 16 (over z, y, core), narrow: 2 (over x).
Axes of the slice: x: 2, y: 2, z: 4, core: 2. Of those that a mesh axis runs over, the one named last changes fastest.
Arguments:
- hidden_in: bfloat16 [16384, 1024], P(('wide', 'narrow')), may hold values from -6 to 6
- segment_ids: int32 [32, 512], P(('wide', 'narrow')), may hold values from 0 to 7, never falling along the last dimension, each value on 1 to 256 neighbouring positions
- expert_ids: int32 [16384, 8], P(('wide', 'narrow')), may hold values from 0 to 15, all different within a row; in each aligned block of 512 rows (0 to 511, 512 to 1023, ...) at most 512 rows name the same one
- attn_gain: float32 [1024], replicated, may hold values from 0.5 to 1.5
- w_query: bfloat16 [1024, 1024], replicated, may hold values from -0.1875 to 0.1875
- w_key: bfloat16 [1024, 512], replicated, may hold values from -0.1875 to 0.1875
- w_value: bfloat16 [1024, 512], replicated, may hold values from -0.1875 to 0.1875
- w_out: bfloat16 [1024, 1024], replicated, may hold values from -0.75 to 0.75
- ffn_gain: float32 [1024], replicated, may hold values from 0.5 to 1.5
- router: bfloat16 [1024, 16], replicated, may hold values from -0.1875 to 0.1875
- w_gate: bfloat16 [16, 1024, 512], P('wide', None, 'narrow'), may hold values from -0.1875 to 0.1875
- w_up: bfloat16 [16, 1024, 512], P('wide', None, 'narrow'), may hold values from -0.1875 to 0.1875
- w_down: bfloat16 [16, 512, 1024], P('wide', 'narrow'), may hold values from -0.75 to 0.75
- grad_out: bfloat16 [16384, 1024], P(('wide', 'narrow')), may hold values from -6 to 6
Outputs:
- hidden_out: bfloat16 [16384, 1024], P(('wide', 'narrow'))
- grad_in: bfloat16 [16384, 1024], P(('wide', 'narrow'))
- grad_attn_gain: float32 [1024], replicated
- grad_query: float32 [1024, 1024], replicated
- grad_key: float32 [1024, 512], replicated
- grad_value: float32 [1024, 512], replicated
- grad_out_proj: float32 [1024, 1024], replicated
- grad_ffn_gain: float32 [1024], replicated
- grad_router: float32 [1024, 16], replicated
- grad_gate: float32 [16, 1024, 512], P('wide', None, 'narrow')
- grad_up: float32 [16, 1024, 512], P('wide', None, 'narrow')
- grad_down: float32 [16, 512, 1024], P('wide', 'narrow')
Inputs may be any that keep to these rules, and one draw needn't show every extreme that they name: `segment_ids`: each packed row has 8 documents numbered in order from 0, each of 1 to half of 512 tokens, one of exactly half of 512. `expert_ids`: each token names 8 different experts. Among the 512 tokens of one packed row no expert is named more than 512 times, and in every draw some row names some expert exactly 512 times.
All inputs are finite; a program needn't handle non-finite values.
Results may differ from a plain program's by a relative error of at most 0.015.
Values may be sent and summed in bfloat16 or wider, within the bound.
A program may use at most 320 MiB of HBM per device.

v0:
```python
import jax
import jax.numpy as jnp
from jax import lax
from jax.sharding import PartitionSpec as P

HD = 64
EPSILON = 1e-05


def norm_scale(values):
    return lax.rsqrt(jnp.mean(values * values, axis=-1, keepdims=True) + EPSILON)


def norm_back(values, inv_rms, gain_vector, grad_rows):
    weighted = grad_rows * gain_vector
    inner = jnp.mean(weighted * values, axis=-1, keepdims=True)
    value_grad = inv_rms * weighted - values * (inv_rms * inv_rms * inv_rms) * inner
    return (value_grad, jnp.sum(grad_rows * values * inv_rms, axis=0))


def rope_tables(length, head_dim):
    half_size = head_dim // 2
    freqs = 10000.0 ** (-(jnp.arange(half_size, dtype=jnp.float32) * 2.0) / head_dim)
    angles = jnp.arange(length, dtype=jnp.float32)[:, None] * freqs[None, :]
    return (jnp.cos(angles), jnp.sin(angles))


def rotate(values, cosine_table, sine_table, direction):
    half_size = values.shape[-1] // 2
    first_half = values[..., :half_size]
    second_half = values[..., half_size:]
    cosine_part = cosine_table[:, None, :]
    sine_part = sine_table[:, None, :] * direction
    return jnp.concatenate(
        [
            first_half * cosine_part - second_half * sine_part,
            second_half * cosine_part + first_half * sine_part,
        ],
        axis=-1,
    )


def attention_probs(grouped, key_rows, allowed, head_dim):
    scores = jnp.einsum(
        "qngd,knd->ngqk", grouped, key_rows, preferred_element_type=jnp.float32
    ) * head_dim ** (-0.5)
    return jnp.where(allowed, scores, -1e30)


def on_device(
    hidden_in,
    segment_ids,
    expert_ids,
    attn_gain,
    w_query,
    w_key,
    w_value,
    w_out,
    ffn_gain,
    router,
    w_gate,
    w_up,
    w_down,
    grad_out,
):
    f32 = jnp.float32
    bf16 = jnp.bfloat16
    length, model_width = hidden_in.shape
    head_dim = HD
    head_count = w_query.shape[1] // head_dim
    kv_count = w_key.shape[1] // head_dim
    group_size = head_count // kv_count
    experts = router.shape[1]
    rows_grad = lax.all_gather(grad_out, "wide", axis=0, tiled=True)
    full_gate, full_up, full_down = (
        lax.all_gather(w_gate, "narrow", axis=2, tiled=True),
        lax.all_gather(w_up, "narrow", axis=2, tiled=True),
        lax.all_gather(w_down, "narrow", axis=1, tiled=True),
    )
    inputs = hidden_in.astype(f32)
    scale_one = norm_scale(inputs)
    normed = (inputs * scale_one * attn_gain).astype(bf16)
    query_pre = jnp.dot(normed, w_query, preferred_element_type=f32)
    key_pre = jnp.dot(normed, w_key, preferred_element_type=f32)
    value_pre = jnp.dot(normed, w_value, preferred_element_type=f32)
    cosine_table, sine_table = rope_tables(length, head_dim)
    query_rows = rotate(
        query_pre.reshape(length, head_count, head_dim), cosine_table, sine_table, 1.0
    ).astype(bf16)
    key_rows = rotate(
        key_pre.reshape(length, kv_count, head_dim), cosine_table, sine_table, 1.0
    ).astype(bf16)
    value_rows = value_pre.astype(bf16).reshape(length, kv_count, head_dim)
    grouped = query_rows.reshape(length, kv_count, group_size, head_dim)
    segments = segment_ids[0]
    places = jnp.arange(length, dtype=jnp.int32)
    allowed = (segments[:, None] == segments[None, :]) & (places[:, None] >= places[None, :])
    scores = attention_probs(grouped, key_rows, allowed, head_dim)
    row_max = jnp.max(scores, axis=-1, keepdims=True)
    log_total = row_max + jnp.log(jnp.sum(jnp.exp(scores - row_max), axis=-1, keepdims=True))
    weights_prob = jnp.exp(scores - log_total)
    attended = jnp.einsum(
        "ngqk,knd->qngd", weights_prob.astype(bf16), value_rows, preferred_element_type=f32
    )
    attended = attended.reshape(length, head_count * head_dim).astype(bf16)
    mixed_rows = inputs + jnp.dot(attended, w_out, preferred_element_type=f32)
    scale_two = norm_scale(mixed_rows)
    ffn_normed = (mixed_rows * scale_two * ffn_gain).astype(bf16)
    logits = jnp.dot(ffn_normed, router, preferred_element_type=f32)
    picked = expert_ids[:, :, None] == jnp.arange(experts, dtype=jnp.int32)[None, None, :]
    member = jnp.any(picked, axis=1)
    masked = jnp.where(member, logits, -jnp.inf)
    powers = jnp.where(member, jnp.exp(masked - jnp.max(masked, axis=-1, keepdims=True)), 0.0)
    gate_probs = powers / jnp.sum(powers, axis=-1, keepdims=True)
    row_gates = lax.all_to_all(gate_probs.T, "wide", split_axis=0, concat_axis=0, tiled=True)
    row_gates = row_gates.reshape(-1, 1)
    rows_in = lax.all_gather(ffn_normed, "wide", axis=0, tiled=True)
    gate_act = jnp.dot(rows_in, full_gate[0], preferred_element_type=f32)
    up_act = jnp.dot(rows_in, full_up[0], preferred_element_type=f32)
    hidden_act = (jax.nn.silu(gate_act) * up_act).astype(bf16)
    outputs = jnp.dot(hidden_act, full_down[0], preferred_element_type=f32).astype(bf16)
    moe_rows = lax.psum_scatter(
        (row_gates * outputs.astype(f32)).astype(bf16), "wide", scatter_dimension=0, tiled=True
    )
    hidden_out = (mixed_rows + moe_rows.astype(f32)).astype(bf16)
    cotangent = grad_out.astype(f32)
    gate_dots = jnp.sum(outputs.astype(f32) * rows_grad.astype(f32), axis=-1)
    gate_grads = lax.all_to_all(
        gate_dots.reshape(experts, length), "wide", split_axis=0, concat_axis=0, tiled=True
    ).T
    logit_grads = (
        gate_probs * (gate_grads - jnp.sum(gate_probs * gate_grads, axis=-1, keepdims=True))
    ).astype(bf16)
    router_grad = jnp.einsum("sd,se->de", ffn_normed, logit_grads, preferred_element_type=f32)
    normed_two_grad = jnp.einsum("se,de->sd", logit_grads, router, preferred_element_type=f32)
    grads_in = (row_gates * rows_grad.astype(f32)).astype(bf16)
    hidden_grad = jnp.einsum("rd,fd->rf", grads_in, full_down[0], preferred_element_type=f32)
    down_w_grad = jnp.einsum("rf,rd->fd", hidden_act, grads_in, preferred_element_type=f32)
    sigmoid_gate = jax.nn.sigmoid(gate_act)
    gate_grad = (
        hidden_grad * up_act * sigmoid_gate * (1.0 + gate_act * (1.0 - sigmoid_gate))
    ).astype(bf16)
    up_grad = (hidden_grad * gate_act * sigmoid_gate).astype(bf16)
    gate_w_grad = jnp.einsum("rd,rf->df", rows_in, gate_grad, preferred_element_type=f32)
    up_w_grad = jnp.einsum("rd,rf->df", rows_in, up_grad, preferred_element_type=f32)
    copy_grads = (
        jnp.einsum("rf,df->rd", gate_grad, full_gate[0], preferred_element_type=f32)
        + jnp.einsum("rf,df->rd", up_grad, full_up[0], preferred_element_type=f32)
    ).astype(bf16)
    rows_back = lax.psum_scatter(copy_grads, "wide", scatter_dimension=0, tiled=True)
    gate_w_grad, up_w_grad, down_w_grad = (
        lax.psum_scatter(
            gate_w_grad[None].astype(jnp.bfloat16), "narrow", scatter_dimension=2, tiled=True
        ).astype(jnp.float32),
        lax.psum_scatter(
            up_w_grad[None].astype(jnp.bfloat16), "narrow", scatter_dimension=2, tiled=True
        ).astype(jnp.float32),
        lax.psum_scatter(
            down_w_grad[None].astype(jnp.bfloat16), "narrow", scatter_dimension=1, tiled=True
        ).astype(jnp.float32),
    )
    normed_two_grad = normed_two_grad + rows_back.astype(f32)
    mixed_part, ffn_gain_grad = norm_back(mixed_rows, scale_two, ffn_gain, normed_two_grad)
    mixed_grad = cotangent + mixed_part
    branch_grad = mixed_grad.astype(bf16)
    out_w_grad = jnp.einsum("sh,sd->hd", attended, branch_grad, preferred_element_type=f32)
    attended_grad = jnp.einsum("sd,hd->sh", branch_grad, w_out, preferred_element_type=f32).astype(
        bf16
    )
    attended_grad = attended_grad.reshape(length, kv_count, group_size, head_dim)
    scores = attention_probs(grouped, key_rows, allowed, head_dim)
    weights_prob = jnp.exp(scores - log_total)
    value_grad = jnp.einsum(
        "ngqk,qngd->knd", weights_prob.astype(bf16), attended_grad, preferred_element_type=f32
    )
    prob_grad = jnp.einsum("qngd,knd->ngqk", attended_grad, value_rows, preferred_element_type=f32)
    score_grad = (
        weights_prob * (prob_grad - jnp.sum(weights_prob * prob_grad, axis=-1, keepdims=True))
    ).astype(bf16)
    query_grad = jnp.einsum(
        "ngqk,knd->qngd", score_grad, key_rows, preferred_element_type=f32
    ) * head_dim ** (-0.5)
    key_grad = jnp.einsum(
        "ngqk,qngd->knd", score_grad, grouped, preferred_element_type=f32
    ) * head_dim ** (-0.5)
    query_grad = rotate(
        query_grad.reshape(length, head_count, head_dim), cosine_table, sine_table, -1.0
    )
    query_grad = query_grad.reshape(length, -1).astype(bf16)
    key_grad = rotate(key_grad, cosine_table, sine_table, -1.0).reshape(length, -1).astype(bf16)
    value_grad = value_grad.reshape(length, -1).astype(bf16)
    query_w_grad = jnp.einsum("sd,sh->dh", normed, query_grad, preferred_element_type=f32)
    key_w_grad = jnp.einsum("sd,sh->dh", normed, key_grad, preferred_element_type=f32)
    value_w_grad = jnp.einsum("sd,sh->dh", normed, value_grad, preferred_element_type=f32)
    normed_one_grad = (
        jnp.einsum("sh,dh->sd", query_grad, w_query, preferred_element_type=f32)
        + jnp.einsum("sh,dh->sd", key_grad, w_key, preferred_element_type=f32)
        + jnp.einsum("sh,dh->sd", value_grad, w_value, preferred_element_type=f32)
    )
    input_part, attn_gain_grad = norm_back(inputs, scale_one, attn_gain, normed_one_grad)
    grad_in = (mixed_grad + input_part).astype(bf16)
    small = jnp.concatenate(
        [
            attn_gain_grad.reshape(-1, 128),
            ffn_gain_grad.reshape(-1, 128),
            router_grad.reshape(-1, 128),
        ],
        axis=0,
    )
    everywhere = ("wide", "narrow")
    columns = jnp.concatenate([query_w_grad, key_w_grad, value_w_grad, out_w_grad], axis=1)
    shares = lax.psum_scatter(columns.astype(bf16), everywhere, scatter_dimension=0, tiled=True)
    columns = lax.all_gather(shares, everywhere, axis=0, tiled=True).astype(f32)
    small = lax.psum(small, everywhere)
    gain_rows = model_width // 128
    query_width, key_width = (w_query.shape[1], w_key.shape[1])
    summed = (
        small[:gain_rows].reshape(-1),
        columns[:, :query_width],
        columns[:, query_width : query_width + key_width],
        columns[:, query_width + key_width : query_width + 2 * key_width],
        columns[:, query_width + 2 * key_width :],
        small[gain_rows : 2 * gain_rows].reshape(-1),
        small[2 * gain_rows :].reshape(router.shape),
    )
    return (
        hidden_out,
        grad_in,
        summed[0],
        summed[1],
        summed[2],
        summed[3],
        summed[4],
        summed[5],
        summed[6],
        gate_w_grad,
        up_w_grad,
        down_w_grad,
    )


def solution(mesh):
    return jax.shard_map(
        on_device,
        mesh=mesh,
        in_specs=(
            P(("wide", "narrow"), None),
            P(("wide", "narrow"), None),
            P(("wide", "narrow"), None),
            P(),
            P(),
            P(),
            P(),
            P(),
            P(),
            P(),
            P("wide", None, "narrow"),
            P("wide", None, "narrow"),
            P("wide", "narrow", None),
            P(("wide", "narrow"), None),
        ),
        out_specs=(
            P(("wide", "narrow"), None),
            P(("wide", "narrow"), None),
            P(),
            P(),
            P(),
            P(),
            P(),
            P(),
            P(),
            P("wide", None, "narrow"),
            P("wide", None, "narrow"),
            P("wide", "narrow", None),
        ),
        check_vma=False,
    )
```

profile of v0, /device:TPU:0, one launch (start us, length us, event | category | flops | bytes accessed | tf_op | source)
XLA Modules:
  0.0 1261.6 jit_solution(9160530426510023094)
XLA Ops:
  17.5 7.8 fusion.83
  25.3 8.2 exponential_reduce_fusion
  33.6 8.5 fusion.25
  51.5 7.3 all-to-all-start
  58.9 116.9 %all-gather.7.cloned.1.call-done = bf16[8192,1024]{1,0:T(8,128)(2,1)} async-done(((bf16[512,1024]{1,0:T(8,128)(2,1)}), bf16[8192,1024]{1,0:T(8,128)(2,1)}) %all-gather.7.cloned.1.call-update) | async-done | bytes 16777232 | tf_op jit(solution)/shard_map/all_gather | solution.py:117
  175.9 16.5 %fusion.47 = f32[8192,512]{1,0:T(8,128)} fusion(bf16[8192,1024]{1,0:T(8,128)(2,1)} %all-gather.7.cloned.1.call-done, bf16[1,1024,512]{2,1,0:T(8,128)(2,1)} %all-gather.11.cloned.1.call-done), kind=kOutput, calls=%fused_computation.74 | convolution fusion | flops 8589934592 | bytes 34603008 | tf_op jit(solution)/shard_map/dot_general | solution.py:119
  192.4 4.5 all-gather.9.cloned.1.call-done
  196.9 16.0 %fusion.51 = f32[8192,512]{1,0:T(8,128)} fusion(bf16[8192,1024]{1,0:T(8,128)(2,1)} %all-gather.7.cloned.1.call-done, bf16[1,1024,512]{2,1,0:T(8,128)(2,1)} %all-gather.9.cloned.1.call-done), kind=kOutput, calls=%fused_computation.78 | convolution fusion | flops 8589934592 | bytes 34603008 | tf_op jit(solution)/shard_map/dot_general | solution.py:118
  212.8 6.7 all-gather.13.cloned.1.call-done
  219.6 128.5 %all-gather.15.cloned.1.call-done = bf16[8192,1024]{1,0:T(8,128)(2,1)} async-done(((bf16[512,1024]{1,0:T(8,128)(2,1)}), bf16[8192,1024]{1,0:T(8,128)(2,1)}) %all-gather.15.cloned.1.call-update) | async-done | bytes 16777232 | tf_op jit(solution)/shard_map/all_gather | solution.py:74
  348.1 32.2 %multiply_convert_fusion = (bf16[8192,512]{1,0:T(8,128)(2,1)}, bf16[8192,512]{1,0:T(8,128)(2,1)}, bf16[8192,512]{1,0:T(8,128)(2,1)}) fusion(f32[8192,512]{1,0:T(8,128)} %fusion.51, f32[8192,512]{1,0:T(8,128)} %fusion.47, bf16[1,512,1024]{2,1,0:T(8,128)(2,1)} %all-gather.13.cloned.1.call-done, bf16[8192,1024]{1,0:T(8,128)(2,1)} %all-gather.15.cloned.1.call-done, ...), kind=kOutput, calls=%fused_computation.13 | convolution fusion | flops 8682209280 | bytes 76578816 | tf_op jit(solution)/shard_map/rd,fd->rf/dot_general | solution.py:137
  380.3 18.8 %fusion.49 = f32[8192,1024]{1,0:T(8,128)} fusion(bf16[8192,512]{1,0:T(8,128)(2,1)} %get-tuple-element.65, bf16[1,1024,512]{2,1,0:T(8,128)(2,1)S(1)} %copy-done.62), kind=kOutput, calls=%fused_computation.76 | convolution fusion | flops 8589934592 | bytes 42991616 | tf_op jit(solution)/shard_map/rf,df->rd/dot_general | solution.py:147
  399.1 21.5 %add_convert_fusion = bf16[8192,1024]{1,0:T(8,128)(2,1)} fusion(f32[8192,1024]{1,0:T(8,128)} %fusion.49, bf16[8192,512]{1,0:T(8,128)(2,1)} %get-tuple-element.64, bf16[1,1024,512]{2,1,0:T(8,128)(2,1)S(1)} %copy-done.60), kind=kOutput, calls=%fused_computation.6 | convolution fusion | flops 8606711808 | bytes 59768832 | tf_op jit(solution)/shard_map/rf,df->rd/dot_general | solution.py:148
  421.9 23.7 %fusion.1 = (f32[8192]{0:T(1024)S(1)}, bf16[8192,1024]{1,0:T(8,128)(2,1)}) fusion(bf16[8192,1024]{1,0:T(8,128)(2,1)} %all-gather.15.cloned.1.call-done, f32[8192]{0:T(1024)S(1)} %bitcast.185, bf16[8192,512]{1,0:T(8,128)(2,1)} %get-tuple-element.66, bf16[1,512,1024]{2,1,0:T(8,128)(2,1)S(1)} %copy-done.61), kind=kOutput, calls=%fused_computation.4 | convolution fusion | flops 8648646656 | bytes 43057152 | tf_op jit(solution)/shard_map/dot_general | solution.py:121
  445.7 9.3 all_to_all.21
  455.1 141.1 %reduce-scatter.11.cloned.1.call-done = bf16[512,1024]{1,0:T(8,128)(2,1)} async-done(((bf16[8192,1024]{1,0:T(8,128)(2,1)}), bf16[512,1024]{1,0:T(8,128)(2,1)}) %reduce-scatter.11.cloned.1.call-update) | async-done | bytes 1048592 | tf_op jit(solution)/shard_map/reduce_scatter | solution.py:150
  600.2 176.6 %reduce-scatter.9.cloned.1.call-done = bf16[512,1024]{1,0:T(8,128)(2,1)} async-done(((bf16[8192,1024]{1,0:T(8,128)(2,1)}), bf16[512,1024]{1,0:T(8,128)(2,1)}) %reduce-scatter.9.cloned.1.call-update) | async-done | bytes 1048592 | tf_op jit(solution)/shard_map/reduce_scatter | solution.py:122
  788.5 9.4 fusion.41
  797.9 16.0 %fusion.3 = (f32[8,2,512]{2,1,0:T(2,128)}, f32[8,512,512,2]{2,1,3,0:T(8,128)}) fusion(f32[8,2,512,512]{2,3,1,0:T(8,128)} %get-tuple-element.93, f32[8,2,512]{2,1,0:T(2,128)S(1)} %bitcast.181, bf16[512,8,64,1]{0,2,3,1:T(8,128)(2,1)} %bitcast.165, bf16[512,8,2,64]{0,3,2,1:T(8,128)(2,1)} %bitcast.160), kind=kOutput, calls=%fused_computation.9 | convolution fusion | flops 549445632 | bytes 35192832 | tf_op jit(solution)/shard_map/qngd,knd->ngqk/dot_general | solution.py:176
  814.0 11.1 fusion.5
  825.1 6.3 fusion.37
  838.8 15.2 %pad_maximum_fusion = bf16[1024,3072]{0,1:T(8,128)(2,1)} fusion(bf16[1024,1024]{0,1:T(8,128)(2,1)S(1)} %copy-done.20, bf16[1024,512]{0,1:T(8,128)(2,1)S(1)} %convolution_convert_fusion.6, bf16[1024,512]{0,1:T(8,128)(2,1)S(1)} %convolution_convert_fusion.7, bf16[1024,1024]{0,1:T(8,128)(2,1)S(1)} %convolution_convert_fusion.1), kind=kLoop, calls=%fused_computation.23 | loop fusion | flops 25165824 | bytes 12582912 | tf_op jit(solution)/shard_map/concatenate | solution.py:211
  854.0 8.7 copy.93
  862.7 15.7 %fusion.32 = bf16[1,1024,512]{2,1,0:T(8,128)(2,1)} fusion(bf16[8192,1024]{1,0:T(8,128)(2,1)} %all-gather.7.cloned.1.call-done, bf16[8192,512]{1,0:T(8,128)(2,1)} %get-tuple-element.64), kind=kOutput, calls=%fused_computation.61 | convolution fusion | flops 8590458880 | bytes 26214400 | tf_op jit(solution)/shard_map/rd,rf->df/dot_general | solution.py:145
  878.5 16.1 %fusion.31 = bf16[1,1024,512]{2,1,0:T(8,128)(2,1)} fusion(bf16[8192,1024]{1,0:T(8,128)(2,1)} %all-gather.7.cloned.1.call-done, bf16[8192,512]{1,0:T(8,128)(2,1)} %get-tuple-element.65), kind=kOutput, calls=%fused_computation.60 | convolution fusion | flops 8590458880 | bytes 26214400 | tf_op jit(solution)/shard_map/rd,rf->df/dot_general | solution.py:144
  895.0 18.9 %fusion.38 = bf16[1,512,1024]{2,1,0:T(8,128)(2,1)} fusion(bf16[8192,512]{1,0:T(8,128)(2,1)} %get-tuple-element.66, bf16[8192,1024]{1,0:T(8,128)(2,1)} %all-gather.15.cloned.1.call-done, f32[8192]{0:T(1024)S(1)} %bitcast.186), kind=kOutput, calls=%fused_computation.66 | convolution fusion | flops 8615624704 | bytes 26247168 | tf_op jit(solution)/shard_map/rf,rd->fd/dot_general | solution.py:138
  925.6 51.4 %reduce-scatter.19.cloned.1.call-done = bf16[32,3072]{1,0:T(8,128)(2,1)} async-done(((bf16[1024,3072]{1,0:T(8,128)(2,1)}), bf16[32,3072]{1,0:T(8,128)(2,1)}) %reduce-scatter.19.cloned.1.call-update) | async-done | bytes 196624 | tf_op jit(solution)/shard_map/reduce_scatter | solution.py:212
  976.9 22.2 %reduce-scatter.15.cloned.1.call-done = bf16[1,1024,256]{2,1,0:T(8,128)(2,1)} async-done(((bf16[1,1024,512]{2,1,0:T(8,128)(2,1)}), bf16[1,1024,256]{2,1,0:T(8,128)(2,1)}) %reduce-scatter.15.cloned.1.call-update) | async-done | bytes 524304 | tf_op jit(solution)/shard_map/reduce_scatter | solution.py:155
  1001.2 21.0 %reduce-scatter.13.cloned.1.call-done = bf16[1,1024,256]{2,1,0:T(8,128)(2,1)} async-done(((bf16[1,1024,512]{2,1,0:T(8,128)(2,1)}), bf16[1,1024,256]{2,1,0:T(8,128)(2,1)}) %reduce-scatter.13.cloned.1.call-update) | async-done | bytes 524304 | tf_op jit(solution)/shard_map/reduce_scatter | solution.py:152
  1024.3 21.2 %reduce-scatter.17.cloned.1.call-done = bf16[1,256,1024]{2,1,0:T(8,128)(2,1)} async-done(((bf16[1,512,1024]{2,1,0:T(8,128)(2,1)}), bf16[1,256,1024]{2,1,0:T(8,128)(2,1)}) %reduce-scatter.17.cloned.1.call-update) | async-done | bytes 524304 | tf_op jit(solution)/shard_map/reduce_scatter | solution.py:158
  1051.4 120.4 %all-reduce.2.cloned.1.call-done = f32[144,128]{1,0:T(8,128)} async-done(((f32[144,128]{1,0:T(8,128)}), f32[144,128]{1,0:T(8,128)}) %all-reduce.2.cloned.1.call-update) | async-done | bytes 73744 | tf_op jit(solution)/shard_map/psum | solution.py:214
  1174.9 71.2 %all-gather.17.cloned.1.call-done = bf16[1024,3072]{1,0:T(8,128)(2,1)} async-done(((bf16[32,3072]{1,0:T(8,128)(2,1)}), bf16[1024,3072]{1,0:T(8,128)(2,1)}) %all-gather.17.cloned.1.call-update) | async-done | bytes 6291472 | tf_op jit(solution)/shard_map/all_gather | solution.py:213
  (214 shorter events, 77.5 us)
Async XLA Ops:
  7.2 34.9 %copy-start = (bf16[1024,1024]{1,0:T(8,128)(2,1)S(1)}, bf16[1024,1024]{1,0:T(8,128)(2,1)}, u32[]{:S(2)}) copy-start(bf16[1024,1024]{1,0:T(8,128)(2,1)} %param.21) | copy-start | bytes 6291460
  7.2 51.7 %all-gather.11.cloned.1.call-start = ((), (), s32[]{:S(2)}) async-start(), calls=%async_computation.10 | async-start | bytes 1572864 | tf_op jit(solution)/shard_map/all_gather | solution.py:77
  8.0 167.9 %all-gather.7.cloned.1.call-start = ((), (), s32[]{:S(2)}) async-start(), calls=%async_computation.8 | async-start | bytes 17825792 | tf_op jit(solution)/shard_map/all_gather | solution.py:117
  14.6 19.0 %copy-start.13 = (bf16[512,512]{0,1:T(8,128)(2,1)}, bf16[512,512]{0,1:T(8,128)(2,1)S(1)}, u32[]{:S(2)}) copy-start(bf16[512,512]{0,1:T(8,128)(2,1)S(1)} %convolution_convert_fusion.8) | copy-start | bytes 1572868
  46.1 150.8 %all-gather.9.cloned.1.call-start = ((), (), s32[]{:S(2)}) async-start(), calls=%async_computation.9 | async-start | bytes 1572864 | tf_op jit(solution)/shard_map/all_gather | solution.py:76
  46.8 172.8 %all-gather.13.cloned.1.call-start = ((), (), s32[]{:S(2)}) async-start(), calls=%async_computation.11 | async-start | bytes 1572864 | tf_op jit(solution)/shard_map/all_gather | solution.py:78
  47.4 300.7 %all-gather.15.cloned.1.call-start = ((), (), s32[]{:S(2)}) async-start(), calls=%async_computation.13 | async-start | bytes 17825792 | tf_op jit(solution)/shard_map/all_gather | solution.py:74
  51.5 161.3 %all-to-all-start = ((f32[16,1,512]{2,1,0:T(1,128)}), f32[16,1,512]{2,1,0:T(1,128)S(1)}, u32[]{:S(2)}, u32[]{:S(2)}) async-start(f32[16,1,512]{2,1,0:T(1,128)} %copy.73), calls=%async_computation | async-start | bytes 65536 | tf_op jit(solution)/shard_map/all_to_all | solution.py:115
  58.9 537.4 %reduce-scatter.11.cloned.1.call-start = ((), (), s32[]{:S(2)}) async-start(), calls=%async_computation.14 | async-start | bytes 17825792 | tf_op jit(solution)/shard_map/reduce_scatter | solution.py:150
  212.8 207.9 %copy-start.50 = (f32[16,1,512]{2,1,0:T(1,128)}, f32[16,1,512]{2,1,0:T(1,128)S(1)}, u32[]{:S(2)}) copy-start(f32[16,1,512]{2,1,0:T(1,128)S(1)} %all-to-all-done) | copy-start | bytes 98308
  348.1 32.2 %copy-start.62 = (bf16[1,1024,512]{2,1,0:T(8,128)(2,1)S(1)}, bf16[1,1024,512]{2,1,0:T(8,128)(2,1)}, u32[]{:S(2)}) copy-start(bf16[1,1024,512]{2,1,0:T(8,128)(2,1)} %all-gather.9.cloned.1.call-done) | copy-start | bytes 3145732
  380.3 18.8 %copy-start.60 = (bf16[1,1024,512]{2,1,0:T(8,128)(2,1)S(1)}, bf16[1,1024,512]{2,1,0:T(8,128)(2,1)}, u32[]{:S(2)}) copy-start(bf16[1,1024,512]{2,1,0:T(8,128)(2,1)} %all-gather.11.cloned.1.call-done) | copy-start | bytes 3145732
  420.7 356.2 %reduce-scatter.9.cloned.1.call-start = ((), (), s32[]{:S(2)}) async-start(), calls=%async_computation.12 | async-start | bytes 17825792 | tf_op jit(solution)/shard_map/reduce_scatter | solution.py:122
  445.6 150.7 %copy-start.41 = (bf16[1024,16]{0,1:T(8,128)(2,1)S(1)}, bf16[1024,16]{0,1:T(8,128)(2,1)}, u32[]{:S(2)}) copy-start(bf16[1024,16]{0,1:T(8,128)(2,1)} %param.23) | copy-start | bytes 98308
  445.6 150.7 %copy-start.47 = (f32[1024]{0:T(1024)S(1)}, f32[1024]{0:T(1024)}, u32[]{:S(2)}) copy-start(f32[1024]{0:T(1024)} %param.22) | copy-start | bytes 12292
  445.6 150.7 %copy-start.49 = (f32[512]{0:T(512)S(1)}, f32[512]{0:T(512)}, u32[]{:S(2)}) copy-start(f32[512]{0:T(512)} %copy-done.48) | copy-start | bytes 6148
  445.7 331.2 %copy-start.10 = (bf16[512,1024]{1,0:T(8,128)(2,1)S(1)}, bf16[512,1024]{1,0:T(8,128)(2,1)}, u32[]{:S(2)}) copy-start(bf16[512,1024]{1,0:T(8,128)(2,1)} %param.27) | copy-start | bytes 3145732
  445.7 331.2 %copy-start.58 = (f32[512]{0:T(512)S(1)}, f32[512]{0:T(512)}, u32[]{:S(2)}) copy-start(f32[512]{0:T(512)} %get-tuple-element.87) | copy-start | bytes 6148
  445.7 531.2 %reduce-scatter.19.cloned.1.call-start = ((), (), s32[]{:S(2)}) async-start(), calls=%async_computation.20 | async-start | bytes 6488064 | tf_op jit(solution)/shard_map/reduce_scatter | solution.py:212
  455.1 326.0 %copy-start.36 = (f32[16,1,512]{2,1,0:T(1,128)}, f32[16,1,512]{2,1,0:T(1,128)S(1)}, u32[]{:S(2)}) copy-start(f32[16,1,512]{2,1,0:T(1,128)S(1)} %all_to_all.21) | copy-start | bytes 98308
  788.5 25.4 %slice-start = ((s8[16777216]{0:T(1024)(128)(4,1)}), s8[4194304]{0:T(1024)(128)(4,1)S(1)}, s32[]{:S(2)}) async-start(s8[16777216]{0:T(1024)(128)(4,1)} %bitcast.157), calls=%async_computation.21 | async-start | bytes 8388608
  788.5 25.4 %slice-start.1 = ((s8[16777216]{0:T(1024)(128)(4,1)}), s8[4194304]{0:T(1024)(128)(4,1)S(1)}, s32[]{:S(2)}) async-start(s8[16777216]{0:T(1024)(128)(4,1)} %bitcast.157), calls=%async_computation.22 | async-start | bytes 8388608
  862.7 136.5 %reduce-scatter.15.cloned.1.call-start = ((), (), s32[]{:S(2)}) async-start(), calls=%async_computation.18 | async-start | bytes 1572864 | tf_op jit(solution)/shard_map/reduce_scatter | solution.py:155
  878.5 16.5 %copy-start.51 = (f32[16,1,512]{2,1,0:T(1,128)S(1)}, f32[16,1,512]{2,1,0:T(1,128)}, u32[]{:S(2)}) copy-start(f32[16,1,512]{2,1,0:T(1,128)} %copy-done.50) | copy-start | bytes 98308
  878.5 143.7 %reduce-scatter.13.cloned.1.call-start = ((), (), s32[]{:S(2)}) async-start(), calls=%async_computation.17 | async-start | bytes 1572864 | tf_op jit(solution)/shard_map/reduce_scatter | solution.py:152
  894.7 19.2 %copy-start.4 = (bf16[512,1024]{1,0:T(8,128)(2,1)S(1)}, bf16[512,1024]{1,0:T(8,128)(2,1)}, u32[]{:S(2)}) copy-start(bf16[512,1024]{1,0:T(8,128)(2,1)} %multiply_convert_fusion.3) | copy-start | bytes 3145732
  894.7 19.2 %copy-start.25 = (f32[512,16]{0,1:T(8,128)S(1)}, f32[512,16]{0,1:T(8,128)}, u32[]{:S(2)}) copy-start(f32[512,16]{0,1:T(8,128)} %copy-done.23) | copy-start | bytes 98308
  894.7 19.2 %copy-start.37 = (f32[16,1,512]{2,1,0:T(1,128)S(1)}, f32[16,1,512]{2,1,0:T(1,128)}, u32[]{:S(2)}) copy-start(f32[16,1,512]{2,1,0:T(1,128)} %copy-done.36) | copy-start | bytes 98308
  894.7 150.8 %reduce-scatter.17.cloned.1.call-start = ((), (), s32[]{:S(2)}) async-start(), calls=%async_computation.19 | async-start | bytes 1572864 | tf_op jit(solution)/shard_map/reduce_scatter | solution.py:158
  913.9 257.9 %all-reduce.2.cloned.1.call-start = ((), (), s32[]{:S(2)}) async-start(), calls=%async_computation.15 | async-start | bytes 147456 | tf_op jit(solution)/shard_map/psum | solution.py:214
  924.6 123.0 %copy-start.57 = (f32[512]{0:T(512)S(1)}, f32[512]{0:T(512)}, u32[]{:S(2)}) copy-start(f32[512]{0:T(512)} %get-tuple-element.85) | copy-start | bytes 6148
  925.3 320.8 %all-gather.17.cloned.1.call-start = ((), (), s32[]{:S(2)}) async-start(), calls=%async_computation.16 | async-start | bytes 6488064 | tf_op jit(solution)/shard_map/all_gather | solution.py:213
  (49 other events, 242.6 us)
Sparse Core Ops, SparseCore 0:
  9.6 23.9 all-gather.10
  46.2 129.6 all-gather.6
  177.4 19.4 all-gather.8
  198.3 21.2 all-gather.12
  221.6 126.4 all-gather.14
  420.8 175.4 reduce-scatter.10
  600.4 176.4 reduce-scatter.8
  862.8 114.0 reduce-scatter.18
  979.7 19.3 reduce-scatter.14
  1001.8 20.3 reduce-scatter.12
  1025.0 20.3 reduce-scatter.16
  1051.5 120.2 all-reduce.1
  1174.7 71.3 all-gather.16
where the time goes:
time: 1270 us; the launch traced here: 1260 us
  waiting for transfers between devices  884 us (70%)
  matrix products  258 us (20%)
  other arithmetic  56.7 us (4%)
  local copies, waits for them, and re-layouts  30 us (2%)
  between operations  15.1 us (1%)
    reduce_scatter x1, waiting for transfers between devices, on_device(): lax.psum_scatter((row_gates * outputs.astype(f32)).astype(bf16), 'wide',...  177 us
    reduce_scatter x1, waiting for transfers between devices, on_device(): lax.psum_scatter(copy_grads, 'wide', scatter_dimension=0, tiled=True)  141 us
    all_gather x1, waiting for transfers between devices, on_device(): rows_grad = lax.all_gather(grad_out, 'wide', axis=0, tiled=True)  128 us
    psum x1, waiting for transfers between devices, on_device(): small = lax.psum(small, everywhere)  120 us
    all_gather x1, waiting for transfers between devices, on_device(): rows_in = lax.all_gather(ffn_normed, 'wide', axis=0, tiled=True)  117 us
    all_gather x1, waiting for transfers between devices, on_device(): columns = lax.all_gather(shares, everywhere, axis=0, tiled=True).astype(f32)  71.2 us
    reduce_scatter x1, waiting for transfers between devices, on_device(): lax.psum_scatter(columns.astype(bf16), everywhere, scatter_dimension=0, t...  51.4 us
    dot_general x1, matrix products, on_device(): jnp.einsum('rd,fd->rf', grads_in, full_down[0], preferred_element_type=f32)  32.2 us
  transfers between devices with their start and end apart: 14, of which 12 were waited for; matrix products, arithmetic and copies ran while one was open for 14% of the time, Pallas kernels for 0%

commit v1 on v0

--- a/solution.py
+++ b/solution.py
@@ -5,6 +5,28 @@
 
 HD = 64
 EPSILON = 1e-05
+
+
+def laid_out(blocks, dim):
+    blocks = jnp.moveaxis(blocks, 0, dim)
+    shape = blocks.shape
+    return blocks.reshape(*shape[:dim], shape[dim] * shape[dim + 1], *shape[dim + 2 :])
+
+
+def collected_by_bits(x, axis):
+    size = lax.axis_size(axis)
+    blocks = x[None]
+    for level in range(size.bit_length() - 1):
+        bit = 1 << level
+        other = lax.ppermute(blocks, axis, [(i, i ^ bit) for i in range(size)])
+        both = jnp.stack([blocks, other])
+        upper = lax.axis_index(axis) >> level & 1
+        blocks = jnp.where(upper == 0, both, both[::-1]).reshape(-1, *x.shape)
+    return blocks
+
+
+def doubled_up(x, axis, dim):
+    return laid_out(collected_by_bits(x, axis), dim)
 
 
 def norm_scale(values):
@@ -114,7 +136,7 @@
     gate_probs = powers / jnp.sum(powers, axis=-1, keepdims=True)
     row_gates = lax.all_to_all(gate_probs.T, "wide", split_axis=0, concat_axis=0, tiled=True)
     row_gates = row_gates.reshape(-1, 1)
-    rows_in = lax.all_gather(ffn_normed, "wide", axis=0, tiled=True)
+    rows_in = doubled_up(ffn_normed, "wide", 0)
     gate_act = jnp.dot(rows_in, full_gate[0], preferred_element_type=f32)
     up_act = jnp.dot(rows_in, full_up[0], preferred_element_type=f32)
     hidden_act = (jax.nn.silu(gate_act) * up_act).astype(bf16)

time: 1270 us -> 1630 us (1.28)
  waiting for transfers between devices: 884 us -> 1190 us
  other arithmetic: 56.7 us -> 109 us
    ppermute x0 -> x4, waiting for transfers between devices: none -> 562 us  [collected_by_bits(): other = lax.ppermute(blocks, axis, [(i, i ^ bit) for i in range(size)])]
    all_gather x1, waiting for transfers between devices: 128 us -> 0.02 us  [on_device(): rows_grad = lax.all_gather(grad_out, 'wide', axis=0, tiled=True)]
    all_gather x1 -> x0, waiting for transfers between devices: 117 us -> none  [on_device(): rows_in = lax.all_gather(ffn_normed, 'wide', axis=0, tiled=True)]
    select_n x0 -> x3, other arithmetic: none -> 28.2 us  [collected_by_bits(): blocks = jnp.where(upper == 0, both, both[::-1]).reshape(-1, *x.shape)]
    another operation x4 -> x10, other arithmetic: 1.06 us -> 25.9 us  [the longest x6 24.9 us: collected_by_bits(): both = jnp.stack([blocks, other])]
    dot_general x1, matrix products: 16 us -> 32.6 us  [on_device(): gate_act = jnp.dot(rows_in, full_gate[0], preferred_element_type=f32)]
  transfers between devices with their start and end apart: 14 -> 17, of which waited for: 12 -> 12; matrix products, arithmetic and copies ran while one was open for 14% -> 14% of each run, Pallas kernels for 0% -> 0%
where the time goes in v1:
time: 1630 us
  waiting for transfers between devices  1190 us (73%)
  matrix products  257 us (16%)
  other arithmetic  109 us (7%)
  local copies, waits for them, and re-layouts  30.9 us (2%)
    ppermute x4, waiting for transfers between devices, collected_by_bits(): other = lax.ppermute(blocks, axis, [(i, i ^ bit) for i in range(size)])  562 us
    reduce_scatter x1, waiting for transfers between devices, on_device(): lax.psum_scatter((row_gates * outputs.astype(f32)).astype(bf16), 'wide',...  176 us
    reduce_scatter x1, waiting for transfers between devices, on_device(): lax.psum_scatter(copy_grads, 'wide', scatter_dimension=0, tiled=True)  141 us
    psum x1, waiting for transfers between devices, on_device(): small = lax.psum(small, everywhere)  121 us
    all_gather x1, waiting for transfers between devices, on_device(): columns = lax.all_gather(shares, everywhere, axis=0, tiled=True).astype(f32)  71 us
    reduce_scatter x1, waiting for transfers between devices, on_device(): lax.psum_scatter(columns.astype(bf16), everywhere, scatter_dimension=0, t...  50.2 us
  transfers between devices with their start and end apart: 17, of which 12 were waited for; matrix products, arithmetic and copies ran while one was open for 14% of the time, Pallas kernels for 0%

profile of v1, /device:TPU:0, one launch (start us, length us, event | category | flops | bytes accessed | tf_op | source)
XLA Modules:
  0.0 1625.6 jit_solution(6333809857060032126)
XLA Ops:
  25.6 8.3 exponential_reduce_fusion
  34.9 8.7 fusion.27
  56.8 57.5 %collective-permute-done.1 = bf16[2,512,1024]{2,1,0:T(8,128)(2,1)} collective-permute-done((bf16[2,512,1024]{2,1,0:T(8,128)(2,1)}, bf16[2,512,1024]{2,1,0:T(8,128)(2,1)}, u32[]{:S(2)}, u32[]{:S(2)}) %collective-permute-start.1) | collective-permute-done | bytes 2097184 | tf_op jit(solution)/shard_map/ppermute | solution.py:21
  122.6 150.5 %collective-permute-done.2 = bf16[4,512,1024]{2,1,0:T(8,128)(2,1)} collective-permute-done((bf16[4,512,1024]{2,1,0:T(8,128)(2,1)}, bf16[4,512,1024]{2,1,0:T(8,128)(2,1)}, u32[]{:S(2)}, u32[]{:S(2)}) %collective-permute-start.2) | collective-permute-done | bytes 4194336 | tf_op jit(solution)/shard_map/ppermute | solution.py:21
  273.1 7.5 pad_maximum_fusion.1
  280.6 14.3 reverse_select_fusion.1
  305.1 353.5 %collective-permute-done.3 = bf16[8,512,1024]{2,1,0:T(8,128)(2,1)} collective-permute-done((bf16[8,512,1024]{2,1,0:T(8,128)(2,1)}, bf16[8,512,1024]{2,1,0:T(8,128)(2,1)}, u32[]{:S(2)}, u32[]{:S(2)}) %collective-permute-start.3) | collective-permute-done | bytes 8388640 | tf_op jit(solution)/shard_map/ppermute | solution.py:21
  658.5 8.0 pad_maximum_fusion
  666.5 10.7 reverse_select_fusion
  677.2 16.0 fusion.49
  693.3 16.1 fusion.9
  709.3 32.6 %multiply_convert_fusion = (bf16[8192,512]{1,0:T(8,128)(2,1)}, bf16[8192,512]{1,0:T(8,128)(2,1)}, bf16[8192,512]{1,0:T(8,128)(2,1)}) fusion(f32[8192,512]{1,0:T(8,128)} %fusion.9, f32[8192,512]{1,0:T(8,128)} %fusion.49, bf16[8192,1024]{1,0:T(8,128)(2,1)} %bitcast.179, bf16[1,1024,512]{2,1,0:T(8,128)(2,1)} %all-gather.6.cloned.1.call-done), kind=kOutput, calls=%fused_computation.15 | convolution fusion | flops 8657043456 | bytes 76546048 | tf_op jit(solution)/shard_map/dot_general | solution.py:140
  741.9 19.0 %fusion.51 = f32[8192,1024]{1,0:T(8,128)} fusion(bf16[8192,512]{1,0:T(8,128)(2,1)} %get-tuple-element.65, bf16[1,1024,512]{2,1,0:T(8,128)(2,1)} %all-gather.6.cloned.1.call-done), kind=kOutput, calls=%fused_computation.86 | convolution fusion | flops 8589934592 | bytes 42991616 | tf_op jit(solution)/shard_map/rf,df->rd/dot_general | solution.py:169
  760.9 21.5 %add_convert_fusion = bf16[8192,1024]{1,0:T(8,128)(2,1)} fusion(f32[8192,1024]{1,0:T(8,128)} %fusion.51, bf16[8192,512]{1,0:T(8,128)(2,1)} %get-tuple-element.64, bf16[1,1024,512]{2,1,0:T(8,128)(2,1)S(1)} %copy-done.61), kind=kOutput, calls=%fused_computation.6 | convolution fusion | flops 8606711808 | bytes 59768832 | tf_op jit(solution)/shard_map/rf,df->rd/dot_general | solution.py:170
  783.6 23.3 %fusion.1 = (f32[8192]{0:T(1024)S(1)}, bf16[8192,1024]{1,0:T(8,128)(2,1)}) fusion(bf16[8192,1024]{1,0:T(8,128)(2,1)} %all-gather.12.cloned.1.call-done, f32[8192]{0:T(1024)S(1)} %bitcast.208, bf16[8192,512]{1,0:T(8,128)(2,1)} %get-tuple-element.66, bf16[1,512,1024]{2,1,0:T(8,128)(2,1)S(1)} %copy-done.60), kind=kOutput, calls=%fused_computation.4 | convolution fusion | flops 8648646656 | bytes 43057152 | tf_op jit(solution)/shard_map/dot_general | solution.py:143
  807.1 11.6 all_to_all.21
  818.7 141.5 %reduce-scatter.11.cloned.1.call-done = bf16[512,1024]{1,0:T(8,128)(2,1)} async-done(((bf16[8192,1024]{1,0:T(8,128)(2,1)}), bf16[512,1024]{1,0:T(8,128)(2,1)}) %reduce-scatter.11.cloned.1.call-update) | async-done | bytes 1048592 | tf_op jit(solution)/shard_map/reduce_scatter | solution.py:172
  964.2 176.5 %reduce-scatter.9.cloned.1.call-done = bf16[512,1024]{1,0:T(8,128)(2,1)} async-done(((bf16[8192,1024]{1,0:T(8,128)(2,1)}), bf16[512,1024]{1,0:T(8,128)(2,1)}) %reduce-scatter.9.cloned.1.call-update) | async-done | bytes 1048592 | tf_op jit(solution)/shard_map/reduce_scatter | solution.py:144
  1152.3 9.4 fusion.43
  1161.7 16.0 fusion.3
  1177.7 11.1 fusion.5
  1202.6 15.1 pad_maximum_fusion.2
  1217.7 8.6 copy.93
  1226.4 15.7 fusion.34
  1242.2 16.1 fusion.33
  1258.6 18.8 %fusion.40 = bf16[1,512,1024]{2,1,0:T(8,128)(2,1)} fusion(bf16[8192,512]{1,0:T(8,128)(2,1)} %get-tuple-element.66, bf16[8192,1024]{1,0:T(8,128)(2,1)} %all-gather.12.cloned.1.call-done, f32[8192]{0:T(1024)S(1)} %bitcast.209), kind=kOutput, calls=%fused_computation.76 | convolution fusion | flops 8615624704 | bytes 26247168 | tf_op jit(solution)/shard_map/rf,rd->fd/dot_general | solution.py:160
  1290.3 50.2 %reduce-scatter.19.cloned.1.call-done = bf16[32,3072]{1,0:T(8,128)(2,1)} async-done(((bf16[1024,3072]{1,0:T(8,128)(2,1)}), bf16[32,3072]{1,0:T(8,128)(2,1)}) %reduce-scatter.19.cloned.1.call-update) | async-done | bytes 196624 | tf_op jit(solution)/shard_map/reduce_scatter | solution.py:234
  1340.5 22.3 %reduce-scatter.15.cloned.1.call-done = bf16[1,1024,256]{2,1,0:T(8,128)(2,1)} async-done(((bf16[1,1024,512]{2,1,0:T(8,128)(2,1)}), bf16[1,1024,256]{2,1,0:T(8,128)(2,1)}) %reduce-scatter.15.cloned.1.call-update) | async-done | bytes 524304 | tf_op jit(solution)/shard_map/reduce_scatter | solution.py:177
  1364.9 21.1 %reduce-scatter.13.cloned.1.call-done = bf16[1,1024,256]{2,1,0:T(8,128)(2,1)} async-done(((bf16[1,1024,512]{2,1,0:T(8,128)(2,1)}), bf16[1,1024,256]{2,1,0:T(8,128)(2,1)}) %reduce-scatter.13.cloned.1.call-update) | async-done | bytes 524304 | tf_op jit(solution)/shard_map/reduce_scatter | solution.py:174
  1388.1 21.0 %reduce-scatter.17.cloned.1.call-done = bf16[1,256,1024]{2,1,0:T(8,128)(2,1)} async-done(((bf16[1,512,1024]{2,1,0:T(8,128)(2,1)}), bf16[1,256,1024]{2,1,0:T(8,128)(2,1)}) %reduce-scatter.17.cloned.1.call-update) | async-done | bytes 524304 | tf_op jit(solution)/shard_map/reduce_scatter | solution.py:180
  1415.0 120.5 %all-reduce.2.cloned.1.call-done = f32[144,128]{1,0:T(8,128)} async-done(((f32[144,128]{1,0:T(8,128)}), f32[144,128]{1,0:T(8,128)}) %all-reduce.2.cloned.1.call-update) | async-done | bytes 73744 | tf_op jit(solution)/shard_map/psum | solution.py:236
  1538.7 71.0 %all-gather.14.cloned.1.call-done = bf16[1024,3072]{1,0:T(8,128)(2,1)} async-done(((bf16[32,3072]{1,0:T(8,128)(2,1)}), bf16[1024,3072]{1,0:T(8,128)(2,1)}) %all-gather.14.cloned.1.call-update) | async-done | bytes 6291472 | tf_op jit(solution)/shard_map/all_gather | solution.py:235
  (227 shorter events, 116.3 us)
Async XLA Ops:
  7.2 36.4 %copy-start = (bf16[1024,1024]{1,0:T(8,128)(2,1)S(1)}, bf16[1024,1024]{1,0:T(8,128)(2,1)}, u32[]{:S(2)}) copy-start(bf16[1024,1024]{1,0:T(8,128)(2,1)} %param.21) | copy-start | bytes 6291460
  7.2 670.0 %all-gather.8.cloned.1.call-start = ((), (), s32[]{:S(2)}) async-start(), calls=%async_computation.9 | async-start | bytes 1572864 | tf_op jit(solution)/shard_map/all_gather | solution.py:99
  8.0 685.3 %all-gather.10.cloned.1.call-start = ((), (), s32[]{:S(2)}) async-start(), calls=%async_computation.10 | async-start | bytes 1572864 | tf_op jit(solution)/shard_map/all_gather | solution.py:100
  8.7 684.5 %all-gather.12.cloned.1.call-start = ((), (), s32[]{:S(2)}) async-start(), calls=%async_computation.12 | async-start | bytes 17825792 | tf_op jit(solution)/shard_map/all_gather | solution.py:96
  11.7 22.3 %copy-start.52 = (f32[512]{0:T(512)}, f32[512]{0:T(512)S(1)}, u32[]{:S(2)}) copy-start(f32[512]{0:T(512)S(1)} %get-tuple-element.88) | copy-start | bytes 6148
  45.6 251.8 %copy-start.46 = (f32[512]{0:T(512)}, f32[512]{0:T(512)S(1)}, u32[]{:S(2)}) copy-start(f32[512]{0:T(512)S(1)} %get-tuple-element.90) | copy-start | bytes 6148
  46.5 3.0 collective-permute-start
  53.8 60.5 %collective-permute-start.1 = (bf16[2,512,1024]{2,1,0:T(8,128)(2,1)}, bf16[2,512,1024]{2,1,0:T(8,128)(2,1)}, u32[]{:S(2)}, u32[]{:S(2)}) collective-permute-start(bf16[2,512,1024]{2,1,0:T(8,128)(2,1)} %get-tuple-element.80), channel_id=1, source_target_pairs={{0,4},{2,6},{4,0},{6,2},{8,12},{10,14},{12,8},{14,10},{16,20},{18,... | collective-permute-start | bytes 6291464 | tf_op jit(solution)/shard_map/ppermute | solution.py:21
  120.8 152.3 %collective-permute-start.2 = (bf16[4,512,1024]{2,1,0:T(8,128)(2,1)}, bf16[4,512,1024]{2,1,0:T(8,128)(2,1)}, u32[]{:S(2)}, u32[]{:S(2)}) collective-permute-start(bf16[4,512,1024]{2,1,0:T(8,128)(2,1)} %bitcast.24), channel_id=1, source_target_pairs={{0,8},{2,10},{4,12},{6,14},{8,0},{10,2},{12,4},{14,6},{16,24},{18,... | collective-permute-start | bytes 12582920 | tf_op jit(solution)/shard_map/ppermute | solution.py:21
  294.9 363.6 %collective-permute-start.3 = (bf16[8,512,1024]{2,1,0:T(8,128)(2,1)}, bf16[8,512,1024]{2,1,0:T(8,128)(2,1)}, u32[]{:S(2)}, u32[]{:S(2)}) collective-permute-start(bf16[8,512,1024]{2,1,0:T(8,128)(2,1)} %bitcast.176), channel_id=1, source_target_pairs={{0,16},{2,18},{4,20},{6,22},{8,24},{10,26},{12,28},{14,30},{16,0},... | collective-permute-start | bytes 25165832 | tf_op jit(solution)/shard_map/ppermute | solution.py:21
  300.9 392.3 %all-to-all-start = ((f32[16,1,512]{2,1,0:T(1,128)}), f32[16,1,512]{2,1,0:T(1,128)S(1)}, u32[]{:S(2)}, u32[]{:S(2)}) async-start(f32[16,1,512]{2,1,0:T(1,128)} %copy.73), calls=%async_computation | async-start | bytes 65536 | tf_op jit(solution)/shard_map/all_to_all | solution.py:137
  304.4 404.9 %all-gather.6.cloned.1.call-start = ((), (), s32[]{:S(2)}) async-start(), calls=%async_computation.8 | async-start | bytes 1572864 | tf_op jit(solution)/shard_map/all_gather | solution.py:98
  305.0 655.2 %reduce-scatter.11.cloned.1.call-start = ((), (), s32[]{:S(2)}) async-start(), calls=%async_computation.13 | async-start | bytes 17825792 | tf_op jit(solution)/shard_map/reduce_scatter | solution.py:172
  693.2 89.3 %copy-start.50 = (f32[16,1,512]{2,1,0:T(1,128)}, f32[16,1,512]{2,1,0:T(1,128)S(1)}, u32[]{:S(2)}) copy-start(f32[16,1,512]{2,1,0:T(1,128)S(1)} %all-to-all-done) | copy-start | bytes 98308
  782.4 358.2 %reduce-scatter.9.cloned.1.call-start = ((), (), s32[]{:S(2)}) async-start(), calls=%async_computation.11 | async-start | bytes 17825792 | tf_op jit(solution)/shard_map/reduce_scatter | solution.py:144
  807.0 153.2 %copy-start.41 = (bf16[1024,16]{0,1:T(8,128)(2,1)S(1)}, bf16[1024,16]{0,1:T(8,128)(2,1)}, u32[]{:S(2)}) copy-start(bf16[1024,16]{0,1:T(8,128)(2,1)} %param.23) | copy-start | bytes 98308
  807.0 153.2 %copy-start.43 = (f32[1024]{0:T(1024)S(1)}, f32[1024]{0:T(1024)}, u32[]{:S(2)}) copy-start(f32[1024]{0:T(1024)} %param.22) | copy-start | bytes 12292
  807.0 153.2 %copy-start.47 = (f32[512]{0:T(512)S(1)}, f32[512]{0:T(512)}, u32[]{:S(2)}) copy-start(f32[512]{0:T(512)} %copy-done.46) | copy-start | bytes 6148
  807.0 333.6 %copy-start.10 = (bf16[512,1024]{1,0:T(8,128)(2,1)S(1)}, bf16[512,1024]{1,0:T(8,128)(2,1)}, u32[]{:S(2)}) copy-start(bf16[512,1024]{1,0:T(8,128)(2,1)} %param.27) | copy-start | bytes 3145732
  807.1 333.6 %copy-start.58 = (f32[512]{0:T(512)S(1)}, f32[512]{0:T(512)}, u32[]{:S(2)}) copy-start(f32[512]{0:T(512)} %get-tuple-element.89) | copy-start | bytes 6148
  807.1 533.4 %reduce-scatter.19.cloned.1.call-start = ((), (), s32[]{:S(2)}) async-start(), calls=%async_computation.19 | async-start | bytes 6488064 | tf_op jit(solution)/shard_map/reduce_scatter | solution.py:234
  818.7 326.2 %copy-start.36 = (f32[16,1,512]{2,1,0:T(1,128)}, f32[16,1,512]{2,1,0:T(1,128)S(1)}, u32[]{:S(2)}) copy-start(f32[16,1,512]{2,1,0:T(1,128)S(1)} %all_to_all.21) | copy-start | bytes 98308
  1152.3 25.4 %slice-start = ((s8[16777216]{0:T(1024)(128)(4,1)}), s8[4194304]{0:T(1024)(128)(4,1)S(1)}, s32[]{:S(2)}) async-start(s8[16777216]{0:T(1024)(128)(4,1)} %bitcast.174), calls=%async_computation.20 | async-start | bytes 8388608
  1152.3 25.4 %slice-start.1 = ((s8[16777216]{0:T(1024)(128)(4,1)}), s8[4194304]{0:T(1024)(128)(4,1)S(1)}, s32[]{:S(2)}) async-start(s8[16777216]{0:T(1024)(128)(4,1)} %bitcast.174), calls=%async_computation.21 | async-start | bytes 8388608
  1226.3 136.5 %reduce-scatter.15.cloned.1.call-start = ((), (), s32[]{:S(2)}) async-start(), calls=%async_computation.17 | async-start | bytes 1572864 | tf_op jit(solution)/shard_map/reduce_scatter | solution.py:177
  1242.1 143.9 %reduce-scatter.13.cloned.1.call-start = ((), (), s32[]{:S(2)}) async-start(), calls=%async_computation.16 | async-start | bytes 1572864 | tf_op jit(solution)/shard_map/reduce_scatter | solution.py:174
  1258.3 19.2 %copy-start.25 = (f32[512,16]{0,1:T(8,128)S(1)}, f32[512,16]{0,1:T(8,128)}, u32[]{:S(2)}) copy-start(f32[512,16]{0,1:T(8,128)} %copy-done.23) | copy-start | bytes 98308
  1258.3 19.2 %copy-start.37 = (f32[16,1,512]{2,1,0:T(1,128)S(1)}, f32[16,1,512]{2,1,0:T(1,128)}, u32[]{:S(2)}) copy-start(f32[16,1,512]{2,1,0:T(1,128)} %copy-done.36) | copy-start | bytes 98308
  1258.3 150.8 %reduce-scatter.17.cloned.1.call-start = ((), (), s32[]{:S(2)}) async-start(), calls=%async_computation.18 | async-start | bytes 1572864 | tf_op jit(solution)/shard_map/reduce_scatter | solution.py:180
  1277.4 258.2 %all-reduce.2.cloned.1.call-start = ((), (), s32[]{:S(2)}) async-start(), calls=%async_computation.14 | async-start | bytes 147456 | tf_op jit(solution)/shard_map/psum | solution.py:236
  1289.3 122.0 %copy-start.57 = (f32[512]{0:T(512)S(1)}, f32[512]{0:T(512)}, u32[]{:S(2)}) copy-start(f32[512]{0:T(512)} %get-tuple-element.87) | copy-start | bytes 6148
  1290.0 319.8 %all-gather.14.cloned.1.call-start = ((), (), s32[]{:S(2)}) async-start(), calls=%async_computation.15 | async-start | bytes 6488064 | tf_op jit(solution)/shard_map/all_gather | solution.py:235
  (51 other events, 321.5 us)
Sparse Core Ops, SparseCore 0:
  9.5 23.9 all-gather.7
  35.1 21.2 all-gather.9
  58.6 180.4 all-gather.11
  306.5 22.4 all-gather.5
  782.6 177.6 reduce-scatter.10
  964.2 176.4 reduce-scatter.8
  1226.4 114.0 reduce-scatter.18
  1343.3 19.4 reduce-scatter.14
  1365.6 20.3 reduce-scatter.12
  1388.7 20.3 reduce-scatter.16
  1415.3 120.2 all-reduce.1
  1538.3 71.3 all-gather.13
